TPU v7x, 64 devices: a 2x2x8 block of a 4x4x8 slice. The times are simulated.
64 devices in a mesh: dp: 4 (over x, y), cp: 16 (over z, core).
Axes of the slice: x: 2, y: 2, z: 8, core: 2. Of those that a mesh axis runs over, the one named last changes fastest.
The devices are a block of a 4x4x8 slice.
Arguments:
- latent: bfloat16 [128, 6, 96, 512], P(('dp', 'cp')), parts along dimension 0
- conv_kernels: bfloat16 [4, 3, 3, 3, 512, 512], replicated
- conv_biases: float32 [4, 512], replicated
- gn_gammas: float32 [4, 512], replicated
- gn_betas: float32 [4, 512], replicated
Outputs:
- output: bfloat16 [128, 6, 96, 512], P(('dp', 'cp')), parts along dimension 0
There are 4 independent parts. A program takes and returns all parts, laid end to end along the dimension named above; an argument that names none is the same for every part.
All inputs are finite; a program needn't handle non-finite values.
Results may differ from a plain program's by a relative error of at most 0.0126155.
Values are sent between devices in bfloat16 or wider.
A program may use at most 768 MiB of HBM per device.

v0:
```python
import jax
import jax.numpy as jnp
from jax import lax
from jax.sharding import PartitionSpec as P

GROUPS = 32
NORM_EPS = 1e-6


def group_sums(hidden):
    n_frames, n_rows, n_cols, n_chans = hidden.shape
    grouped = hidden.astype(jnp.float32).reshape(n_frames, n_rows, n_cols, GROUPS, n_chans // GROUPS)
    return jnp.stack([jnp.sum(grouped, axis=(0, 1, 2, 4)), jnp.sum(grouped * grouped, axis=(0, 1, 2, 4))])


def norm_act(hidden, grp_sums, elem_count, gn_gamma, gn_beta):
    grp_mean = grp_sums[0] / elem_count
    grp_var = grp_sums[1] / elem_count - grp_mean * grp_mean
    group_width = hidden.shape[-1] // GROUPS
    chan_scale = jnp.repeat(lax.rsqrt(grp_var + NORM_EPS), group_width) * gn_gamma
    chan_shift = gn_beta - jnp.repeat(grp_mean, group_width) * chan_scale
    normed = (hidden.astype(jnp.float32) * chan_scale + chan_shift).astype(jnp.bfloat16)
    return jax.nn.silu(normed.astype(jnp.float32)).astype(jnp.bfloat16)


def conv_frames(padded, kernel, conv_bias):
    result = lax.conv_general_dilated(padded[None], kernel, window_strides=(1, 1, 1), padding=((0, 0), (1, 1), (1, 1)), dimension_numbers=("NDHWC", "DHWIO", "NDHWC"), preferred_element_type=jnp.float32)[0]
    return (result + conv_bias).astype(jnp.bfloat16)


def solution(mesh):
    n_time = mesh.shape["cp"]
    next_perm = [(src, src + 1) for src in range(n_time - 1)]
    frame_spec = P(("dp", "cp"))

    def local_fn(latent, conv_kernels, conv_biases, gn_gammas, gn_betas):
        n_frames, n_rows, n_cols, n_chans = latent.shape
        my_rank = lax.axis_index("cp")
        elem_count = n_time * n_frames * n_rows * n_cols * (n_chans // GROUPS)

        def gn_step(hidden, layer_idx):
            grp_sums = lax.psum(group_sums(hidden), "cp")
            return norm_act(hidden, grp_sums, elem_count, gn_gammas[layer_idx], gn_betas[layer_idx])

        def conv_step(act_in, layer_idx):
            from_prev = lax.ppermute(act_in[n_frames - 2:], "cp", next_perm)
            own_first = jnp.concatenate([act_in[:1], act_in[:1]], axis=0)
            halo_frames = jnp.where(my_rank == 0, own_first, from_prev)
            return conv_frames(jnp.concatenate([halo_frames, act_in], axis=0), conv_kernels[layer_idx], conv_biases[layer_idx])

        hidden = latent
        for block_idx in range(2):
            first_layer = 2 * block_idx
            inner = conv_step(gn_step(hidden, first_layer), first_layer)
            inner = conv_step(gn_step(inner, first_layer + 1), first_layer + 1)
            hidden = (hidden.astype(jnp.float32) + inner.astype(jnp.float32)).astype(jnp.bfloat16)
        return hidden

    return jax.shard_map(local_fn, mesh=mesh, in_specs=(frame_spec, P(), P(), P(), P()), out_specs=frame_spec, check_vma=False)
```

profile of v0, /device:TPU:150, one launch (start us, length us, event | category | flops | bytes accessed | tf_op | source)
XLA Modules:
  0.0 310.9 jit_solution(16338992723605355873)
XLA Ops:
  2.1 23.6 %psum.28 = f32[2,32]{1,0:T(2,128)S(1)} all-reduce(f32[2,32]{1,0:T(2,128)S(1)} %pad_maximum_fusion), channel_id=1, replica_groups=mesh['dp'=4,'cp'=16] {'cp'}, use_global_device_ids=true, to_apply=%region_4.5 | all-reduce | flops 64 | bytes 512 | tf_op jit(solution)/shard_map/psum | solution.py:42
  27.8 1.9 fusion.49
  29.7 2.0 collective-permute-start
  32.3 16.1 %collective-permute-done = bf16[2,6,96,512]{3,2,1,0:T(8,128)(2,1)S(1)} collective-permute-done((bf16[2,6,96,512]{3,2,1,0:T(8,128)(2,1)S(1)}, bf16[2,6,96,512]{3,2,1,0:T(8,128)(2,1)S(1)}, u32[]{:S(2)}, u32[]{:S(2)}) %collective-permute-start) | collective-permute-done | bytes 1179680 | tf_op jit(solution)/shard_map/ppermute | solution.py:46
  48.8 1.8 copy.44
  52.3 24.8 %fusion.40 = (f32[512]{0:T(512)S(1)}, f32[512]{0:T(512)S(1)}, f32[2,6,8,13,512]{4,2,3,1,0:T(8,128)S(1)}) fusion(pred[8,13]{0,1:T(8,128)(4,1)S(1)} %copy-done.3, f32[512]{0:T(512)S(1)} %bitcast.169, bf16[4,3,3,3,512,512]{5,4,3,2,1,0:T(8,128)(2,1)} %param.6, bf16[4,6,1,7,2,512]{5,3,4,1,0,2:T(8,128)(2,1)S(1)} %slice.125, ...), kind=kOutput, calls=%fused_computation.57 | convolution fusion | flops 15718072320 | bytes 19617896 | tf_op jit(solution)/shard_map/conv_general_dilated | solution.py:27
  77.6 23.9 %psum.29 = f32[2,32]{1,0:T(2,128)S(1)} all-reduce(f32[2,32]{1,0:T(2,128)S(1)} %pad_maximum_fusion.1), channel_id=1, replica_groups=mesh['dp'=4,'cp'=16] {'cp'}, use_global_device_ids=true, to_apply=%region_9.10 | all-reduce | flops 64 | bytes 512 | tf_op jit(solution)/shard_map/psum | solution.py:42
  101.8 2.0 copy.23
  105.4 2.0 collective-permute-start.1
  107.4 16.7 %collective-permute-done.1 = bf16[2,6,96,512]{3,2,1,0:T(8,128)(2,1)S(1)} collective-permute-done((bf16[2,6,96,512]{3,2,1,0:T(8,128)(2,1)S(1)}, bf16[2,6,96,512]{3,2,1,0:T(8,128)(2,1)S(1)}, u32[]{:S(2)}, u32[]{:S(2)}) %collective-permute-start.1) | collective-permute-done | bytes 1179680 | tf_op jit(solution)/shard_map/ppermute | solution.py:46
  124.5 1.8 copy.45
  127.9 25.5 %fusion.87 = f32[2,6,8,13,512]{4,2,3,1,0:T(8,128)S(1)} fusion(bf16[4,3,3,3,512,512]{5,4,3,2,1,0:T(8,128)(2,1)} %param.6, bf16[4,6,1,7,2,512]{5,3,4,1,0,2:T(8,128)(2,1)S(1)} %slice.128, bf16[4,6,1,8,13,512]{5,3,4,1,0,2:T(8,128)(2,1)S(1)} %copy.27, pred[8,13]{0,1:T(8,128)(4,1)S(1)} %copy-done.3), kind=kOutput, calls=%fused_computation.112 | convolution fusion | flops 15712960512 | bytes 19611752 | tf_op jit(solution)/shard_map/conv_general_dilated | solution.py:27
  153.4 2.0 copy.28
  157.7 23.6 %psum.30 = f32[2,32]{1,0:T(2,128)S(1)} all-reduce(f32[2,32]{1,0:T(2,128)S(1)} %pad_maximum_fusion.2), channel_id=1, replica_groups=mesh['dp'=4,'cp'=16] {'cp'}, use_global_device_ids=true, to_apply=%region_14.15 | all-reduce | flops 64 | bytes 512 | tf_op jit(solution)/shard_map/psum | solution.py:42
  182.4 2.0 collective-permute-start.2
  184.4 16.8 %collective-permute-done.2 = bf16[2,6,96,512]{3,2,1,0:T(8,128)(2,1)S(1)} collective-permute-done((bf16[2,6,96,512]{3,2,1,0:T(8,128)(2,1)S(1)}, bf16[2,6,96,512]{3,2,1,0:T(8,128)(2,1)S(1)}, u32[]{:S(2)}, u32[]{:S(2)}) %collective-permute-start.2) | collective-permute-done | bytes 1179680 | tf_op jit(solution)/shard_map/ppermute | solution.py:46
  201.5 1.8 copy.46
  204.9 23.5 %fusion.43 = (f32[512]{0:T(512)S(1)}, f32[512]{0:T(512)S(1)}, f32[2,6,8,13,512]{4,2,3,1,0:T(8,128)}) fusion(pred[8,13]{0,1:T(8,128)(4,1)S(1)} %copy-done.3, f32[512]{0:T(512)S(1)} %bitcast.167, bf16[4,3,3,3,512,512]{5,4,3,2,1,0:T(8,128)(2,1)} %param.6, bf16[4,6,1,7,2,512]{5,3,4,1,0,2:T(8,128)(2,1)S(1)} %slice.131, bf16[4,6,1,8,13,512]{5,3,4,1,0,2:T(8,128)(2,1)S(1)} %copy.32), kind=kOutput, calls=%fused_computation.60 | convolution fusion | flops 15718072320 | bytes 19617896 | tf_op jit(solution)/shard_map/conv_general_dilated | solution.py:27
  228.8 24.0 %psum.31 = f32[2,32]{1,0:T(2,128)S(1)} all-reduce(f32[2,32]{1,0:T(2,128)S(1)} %pad_maximum_fusion.3), channel_id=1, replica_groups=mesh['dp'=4,'cp'=16] {'cp'}, use_global_device_ids=true, to_apply=%region_19.20 | all-reduce | flops 64 | bytes 512 | tf_op jit(solution)/shard_map/psum | solution.py:42
  253.2 3.7 %copy.33 = f32[2,6,8,13,512]{4,0,3,2,1:T(2,128)S(1)} copy(f32[2,6,8,13,512]{4,2,3,1,0:T(8,128)} %get-tuple-element.35) | data formatting | bytes 5111808 | tf_op jit(solution)/shard_map/conv_general_dilated | solution.py:27
  258.5 2.0 collective-permute-start.3
  260.5 16.7 %collective-permute-done.3 = bf16[2,6,96,512]{3,2,1,0:T(8,128)(2,1)S(1)} collective-permute-done((bf16[2,6,96,512]{3,2,1,0:T(8,128)(2,1)S(1)}, bf16[2,6,96,512]{3,2,1,0:T(8,128)(2,1)S(1)}, u32[]{:S(2)}, u32[]{:S(2)}) %collective-permute-start.3) | collective-permute-done | bytes 1179680 | tf_op jit(solution)/shard_map/ppermute | solution.py:46
  281.0 25.3 %fusion.97 = f32[2,6,8,13,512]{4,2,3,1,0:T(8,128)S(1)} fusion(bf16[4,3,3,3,512,512]{5,4,3,2,1,0:T(8,128)(2,1)} %param.6, bf16[4,6,1,7,2,512]{5,3,4,1,0,2:T(8,128)(2,1)S(1)} %slice.134, bf16[4,6,1,8,13,512]{5,3,4,1,0,2:T(8,128)(2,1)S(1)} %copy.37, pred[8,13]{0,1:T(8,128)(4,1)S(1)} %copy-done.3), kind=kOutput, calls=%fused_computation.114 | convolution fusion | flops 15712960512 | bytes 19611752 | tf_op jit(solution)/shard_map/conv_general_dilated | solution.py:27
  306.3 2.0 copy.38
  (94 shorter events, 24.6 us)
Async XLA Ops:
  0.0 31.7 %copy-start.2 = (f32[4,512]{1,0:T(4,128)S(1)}, f32[4,512]{1,0:T(4,128)}, u32[]{:S(2)}) copy-start(f32[4,512]{1,0:T(4,128)} %param.7) | copy-start | bytes 24580
  29.7 18.8 %collective-permute-start = (bf16[2,6,96,512]{3,2,1,0:T(8,128)(2,1)S(1)}, bf16[2,6,96,512]{3,2,1,0:T(8,128)(2,1)S(1)}, u32[]{:S(2)}, u32[]{:S(2)}) collective-permute-start(bf16[2,6,96,512]{3,2,1,0:T(8,128)(2,1)S(1)} %fusion.49), channel_id=1, source_target_pairs={{0,1},{1,2},{2,3},{3,4},{4,5},{5,6},{6,7},{7,8},{8,9},{9,10},{10,1... | collective-permute-start | bytes 3538952 | tf_op jit(solution)/shard_map/ppermute | solution.py:46
  51.6 0.7 copy-start.3
  105.4 18.8 %collective-permute-start.1 = (bf16[2,6,96,512]{3,2,1,0:T(8,128)(2,1)S(1)}, bf16[2,6,96,512]{3,2,1,0:T(8,128)(2,1)S(1)}, u32[]{:S(2)}, u32[]{:S(2)}) collective-permute-start(bf16[2,6,96,512]{3,2,1,0:T(8,128)(2,1)S(1)} %fusion.53), channel_id=1, source_target_pairs={{0,1},{1,2},{2,3},{3,4},{4,5},{5,6},{6,7},{7,8},{8,9},{9,10},{10,1... | collective-permute-start | bytes 3538952 | tf_op jit(solution)/shard_map/ppermute | solution.py:46
  155.4 1.3 copy-start
  182.4 18.8 %collective-permute-start.2 = (bf16[2,6,96,512]{3,2,1,0:T(8,128)(2,1)S(1)}, bf16[2,6,96,512]{3,2,1,0:T(8,128)(2,1)S(1)}, u32[]{:S(2)}, u32[]{:S(2)}) collective-permute-start(bf16[2,6,96,512]{3,2,1,0:T(8,128)(2,1)S(1)} %fusion.57), channel_id=1, source_target_pairs={{0,1},{1,2},{2,3},{3,4},{4,5},{5,6},{6,7},{7,8},{8,9},{9,10},{10,1... | collective-permute-start | bytes 3538952 | tf_op jit(solution)/shard_map/ppermute | solution.py:46
  258.5 18.8 %collective-permute-start.3 = (bf16[2,6,96,512]{3,2,1,0:T(8,128)(2,1)S(1)}, bf16[2,6,96,512]{3,2,1,0:T(8,128)(2,1)S(1)}, u32[]{:S(2)}, u32[]{:S(2)}) collective-permute-start(bf16[2,6,96,512]{3,2,1,0:T(8,128)(2,1)S(1)} %fusion.61), channel_id=1, source_target_pairs={{0,1},{1,2},{2,3},{3,4},{4,5},{5,6},{6,7},{7,8},{8,9},{9,10},{10,1... | collective-permute-start | bytes 3538952 | tf_op jit(solution)/shard_map/ppermute | solution.py:46
  308.3 0.8 copy-start.1
where the time goes:
time: 316 us; the launch traced here: 311 us
  matrix products  99.1 us (31%)
  blocking collectives  95.2 us (30%)
  waiting for transfers between devices  66.4 us (21%)
  local copies, waits for them, and re-layouts  31.3 us (10%)
  other arithmetic  10.4 us (3%)
  starting transfers between devices  7.8 us (2%)
    conv_general_dilated x4, matrix products, conv_frames(): lax.conv_general_dilated(padded[None], kernel, window_strides=(1, 1, 1),...  99.1 us
    psum x4, blocking collectives, gn_step(): grp_sums = lax.psum(group_sums(hidden), 'cp')  95.2 us
    ppermute x4, waiting for transfers between devices, conv_step(): from_prev = lax.ppermute(act_in[n_frames - 2:], 'cp', next_perm)  66.4 us
    conv_general_dilated x16, local copies, waits for them, and re-layouts, conv_frames(): lax.conv_general_dilated(padded[None], kernel, window_strides=(1, 1, 1),...  15.3 us
    unnamed x12, local copies, waits for them, and re-layouts  7.82 us
    ppermute x4, starting transfers between devices, conv_step(): from_prev = lax.ppermute(act_in[n_frames - 2:], 'cp', next_perm)  7.8 us
  transfers between devices with their start and end apart: 4, of which 4 were waited for; matrix products, arithmetic and copies ran while one was open for 0% of the time, Pallas kernels for 0%

commit v1 on v0

v1 whole, which is shorter than its diff:
```python
import functools

import jax
import jax.numpy as jnp
from jax import lax
from jax.experimental import pallas as pl
from jax.experimental.pallas import tpu as pltpu
from jax.sharding import PartitionSpec as P

GROUPS = 32
NORM_EPS = 1e-6
F32 = jnp.float32
BF16 = jnp.bfloat16
MESH = pl.DeviceIdType.MESH
TILE = 256
LANES = 128


def _kernel(n_time, n_layers, n_rows, n_cols, n_chans, elem_count,
            x_hbm, w_hbm, bias_ref, gamma_ref, beta_ref, out_hbm,
            raw, xres, act_h0, act_h1, act_a0, act_a1, wbuf, accs, st, ss, stat_tx, stat_rx,
            x_sems, w_sems, halo_send, halo_recv, stat_send, stat_recv, out_sems):
    dp = lax.axis_index("dp")
    me = lax.axis_index("cp")
    acts = (act_h0, act_h1, act_a0, act_a1)
    n_blk = n_chans // LANES
    n_half = n_chans // TILE
    frame_rows = n_rows * n_cols
    group_width = n_chans // GROUPS
    has_next = me < n_time - 1
    has_prev = me > 0
    half_rows = n_rows // 2

    def peer(dist):
        return lax.rem(me + dist, n_time)

    def halo_copy(src, parity, t):
        return pltpu.make_async_remote_copy(
            src_ref=src, dst_ref=raw.at[2 + 2 * parity + t], send_sem=halo_send.at[t],
            recv_sem=halo_recv.at[parity, t], device_id=(dp, lax.rem(me + 1, n_time)), device_id_type=MESH)

    def weight_copy(layer, parity, k):
        return pltpu.make_async_copy(w_hbm.at[layer, k], wbuf.at[parity, k], w_sems.at[parity, k])

    def stat_copy(parity, dist):
        return pltpu.make_async_remote_copy(
            src_ref=stat_tx.at[parity], dst_ref=stat_rx.at[parity, me], send_sem=stat_send.at[parity, dist],
            recv_sem=stat_recv.at[parity, me], device_id=(dp, peer(dist)), device_id_type=MESH)

    def stat_arrival(parity, dist):
        return pltpu.make_async_remote_copy(
            src_ref=stat_tx.at[parity], dst_ref=stat_rx.at[parity, peer(dist)], send_sem=stat_send.at[parity, dist],
            recv_sem=stat_recv.at[parity, peer(dist)], device_id=(dp, peer(dist)), device_id_type=MESH)

    far_first = sorted(range(1, n_time), key=lambda d: -min(d, n_time - d))

    def send_stats(parity):
        for row in range(2):
            total = jnp.sum(st[row], axis=0, keepdims=True)
            for blk in range(n_blk):
                stat_tx[parity, row * n_blk + blk:row * n_blk + blk + 1, :] = total[:, blk * LANES:(blk + 1) * LANES]
        stat_rx[parity, me] = stat_tx[parity]
        for dist in far_first:
            stat_copy(parity, dist).start()

    def finish_stats(layer, parity):
        for dist in range(1, n_time):
            stat_arrival(parity, dist).wait_recv()
        for dist in range(1, n_time):
            stat_copy(parity, dist).wait_send()
        total = stat_rx[parity, 0]
        for src in range(1, n_time):
            total = total + stat_rx[parity, src]
        lane = lax.broadcasted_iota(jnp.int32, total.shape, 1)
        step = 1
        while step < group_width:
            other = jnp.where((lane & step) != 0, pltpu.roll(total, step, 1), pltpu.roll(total, LANES - step, 1))
            total = total + other
            step *= 2
        mean = total[:n_blk] / elem_count
        var = total[n_blk:] / elem_count - mean * mean
        scale = lax.rsqrt(var + NORM_EPS) * gamma_ref[layer]
        shift = beta_ref[layer] - mean * scale
        for blk in range(n_blk):
            ss[0:1, blk * LANES:(blk + 1) * LANES] = scale[blk:blk + 1]
            ss[1:2, blk * LANES:(blk + 1) * LANES] = shift[blk:blk + 1]

    def add_stats(val, lanes):
        grouped = val.reshape(val.shape[0] // 8, 8, val.shape[1])
        st[0, :, lanes] += jnp.sum(grouped, axis=0)
        st[1, :, lanes] += jnp.sum(grouped * grouped, axis=0)

    def norm_item(src_idx, act, row, blk):
        rows = slice(row * n_cols, (row + 1) * n_cols)
        lanes = slice(blk * LANES, (blk + 1) * LANES)
        val = raw[src_idx, rows, lanes].astype(F32)
        val = (val * ss[0:1, lanes] + ss[1:2, lanes]).astype(BF16).astype(F32)
        val = val * lax.logistic(val)
        col = lax.broadcasted_iota(jnp.int32, val.shape, 0)
        act[rows, n_chans + blk * LANES:n_chans + (blk + 1) * LANES] = val.astype(BF16)
        before = jnp.where(col == 0, 0.0, pltpu.roll(val, 1, 0))
        act[rows, blk * LANES:(blk + 1) * LANES] = before.astype(BF16)
        after = jnp.where(col == n_cols - 1, 0.0, pltpu.roll(val, n_cols - 1, 0))
        act[rows, 2 * n_chans + blk * LANES:2 * n_chans + (blk + 1) * LANES] = after.astype(BF16)

    def norm_items(src_idx, act, blks):
        return [functools.partial(norm_item, src_idx, act, row, blk) for blk in blks for row in range(n_rows)]

    def run_body(accs):
        def pop_item(layer, odd, t, row, q):
            rows = slice(row * n_cols, (row + 1) * n_cols)
            lanes = slice(q * TILE, (q + 1) * TILE)
            val = accs[t, rows, lanes] + bias_ref[layer, 0:1, lanes]
            val = val.astype(BF16).astype(F32)
            val = val + xres[0, t, rows, lanes].astype(F32) * odd.astype(F32)
            val = val.astype(BF16)
            raw[t, rows, lanes] = val
            xres[1 - odd, t, rows, lanes] = val
            add_stats(val.astype(F32), lanes)

        def group(parity, k, act, t, rows, first, items):
            lo, hi = rows[0], rows[-1] + 1
            done = 0
            parts = {}
            for idx, di in enumerate((0, -1, 1)):
                r0, r1 = max(lo, -di), min(hi, n_rows - di)
                weight = wbuf[parity, k, (di + 1) * 3 * n_chans:(di + 2) * 3 * n_chans, :]
                prod = jnp.dot(act[(r0 + di) * n_cols:(r1 + di) * n_cols, :], weight, preferred_element_type=F32)
                for row in range(r0, r1):
                    piece = prod[(row - r0) * n_cols:(row - r0 + 1) * n_cols]
                    parts[row] = piece if row not in parts else parts[row] + piece
                upto = (len(items) * (idx + 1)) // 3
                for item in items[done:upto]:
                    item()
                done = upto
            for row in range(lo, hi):
                here = slice(row * n_cols, (row + 1) * n_cols)
                if first:
                    accs[t, here, :] = parts[row]
                else:
                    accs[t, here, :] += parts[row]

        whole = range(n_rows)

        def pops(layer, odd, t, rows):
            return [functools.partial(pop_item, layer, odd, t, row, q) for row in rows for q in range(n_half)]

        barrier = pltpu.get_barrier_semaphore()
        for dist in range(1, n_time):
            pl.semaphore_signal(barrier, inc=1, device_id=(dp, peer(dist)), device_id_type=MESH)
        for t in (1, 0):
            pltpu.make_async_copy(x_hbm.at[t], raw.at[t], x_sems.at[t]).start()
        for k in (2, 1, 0):
            weight_copy(0, 0, k).start()
        for t in (1, 0):
            pltpu.make_async_copy(x_hbm.at[t], xres.at[0, t], x_sems.at[2 + t]).start()
        st[...] = jnp.zeros_like(st)
        for t in (1, 0):
            pltpu.make_async_copy(x_hbm.at[t], raw.at[t], x_sems.at[t]).wait()

            def stat_rows(i, carry, t=t):
                base = pl.multiple_of(i * n_cols, n_cols)
                for q in range(n_half):
                    lanes = slice(q * TILE, (q + 1) * TILE)
                    add_stats(raw[t, pl.ds(base, n_cols), lanes].astype(F32), lanes)
                return carry

            lax.fori_loop(0, n_rows, stat_rows, 0)
        pl.semaphore_wait(barrier, n_time - 1)
        send_stats(0)

        @pl.when(has_next)
        def _():
            for t in (1, 0):
                halo_copy(x_hbm.at[t], 0, t).start()

        def layer_step(layer, carry):
            parity = lax.rem(layer, 2)
            odd = parity
            nxt = 1 - parity
            more = layer < n_layers - 1

            @pl.when(more)
            def _():
                for k in (2, 1, 0):
                    weight_copy(layer + 1, nxt, k).start()

            finish_stats(layer, parity)
            st[...] = jnp.zeros_like(st)
            first_half = range(n_blk // 2)
            second_half = range(n_blk // 2, n_blk)
            for item in norm_items(1, act_a1, first_half):
                item()
            weight_copy(layer, parity, 2).wait()
            for item in norm_items(1, act_a1, second_half):
                item()
            group(parity, 2, act_a1, 1, whole, True, norm_items(0, act_a0, range(n_blk)))

            weight_copy(layer, parity, 1).wait()

            @pl.when(has_prev)
            def _():
                halo_copy(raw.at[1], parity, 1).wait_recv()

            src1 = jnp.where(has_prev, 3 + 2 * parity, 0)
            src0 = jnp.where(has_prev, 2 + 2 * parity, 0)
            group(parity, 1, act_a0, 1, whole, False, norm_items(src1, act_h1, range(n_blk)))

            weight_copy(layer, parity, 0).wait()

            @pl.when(has_next)
            def _():
                halo_copy(raw.at[1], nxt, 1).wait_send()

            @pl.when(layer == 0)
            def _():
                for t in (1, 0):
                    pltpu.make_async_copy(x_hbm.at[t], xres.at[0, t], x_sems.at[2 + t]).wait()

            group(parity, 0, act_h1, 1, whole, False, [])

            @pl.when(has_prev)
            def _():
                halo_copy(raw.at[0], parity, 0).wait_recv()

            for item in pops(layer, odd, 1, whole):
                item()

            @pl.when(jnp.logical_and(more, has_next))
            def _():
                halo_copy(raw.at[1], nxt, 1).start()

            @pl.when(jnp.logical_not(more))
            def _():
                pltpu.make_async_copy(raw.at[1], out_hbm.at[1], out_sems.at[1]).start()

            group(parity, 2, act_a0, 0, whole, True, norm_items(src0, act_h0, range(n_blk)))
            group(parity, 1, act_h1, 0, whole, False, [])

            @pl.when(has_next)
            def _():
                halo_copy(raw.at[0], nxt, 0).wait_send()

            group(parity, 0, act_h0, 0, whole, False, [])
            for item in pops(layer, odd, 0, whole):
                item()

            @pl.when(more)
            def _():
                send_stats(nxt)

            @pl.when(jnp.logical_and(more, has_next))
            def _():
                halo_copy(raw.at[0], nxt, 0).start()

            @pl.when(jnp.logical_not(more))
            def _():
                pltpu.make_async_copy(raw.at[0], out_hbm.at[0], out_sems.at[0]).start()

            return carry

        lax.fori_loop(0, n_layers, layer_step, 0)
        for t in (1, 0):
            pltpu.make_async_copy(raw.at[t], out_hbm.at[t], out_sems.at[t]).wait()

    run_body(accs)


def solution(mesh):
    n_time = mesh.shape["cp"]
    frame_spec = P(("dp", "cp"))

    def local_fn(latent, conv_kernels, conv_biases, gn_gammas, gn_betas):
        n_frames, n_rows, n_cols, n_chans = latent.shape
        n_layers = conv_kernels.shape[0]
        n_taps = conv_kernels.shape[1]
        n_blk = n_chans // LANES
        elem_count = n_time * n_frames * n_rows * n_cols * (n_chans // GROUPS)
        frame = (n_rows * n_cols, n_chans)
        any_spec = pl.BlockSpec(memory_space=pl.ANY)
        vmem_spec = pl.BlockSpec(memory_space=pltpu.VMEM)
        decoded = pl.pallas_call(
            functools.partial(_kernel, n_time, n_layers, n_rows, n_cols, n_chans, float(elem_count)),
            out_shape=jax.ShapeDtypeStruct((n_frames,) + frame, BF16),
            in_specs=[any_spec, any_spec, vmem_spec, vmem_spec, vmem_spec],
            out_specs=any_spec,
            scratch_shapes=[
                pltpu.VMEM((6,) + frame, BF16),
                pltpu.VMEM((2, n_frames) + frame, BF16),
                pltpu.VMEM((frame[0], 3 * n_chans), BF16),
                pltpu.VMEM((frame[0], 3 * n_chans), BF16),
                pltpu.VMEM((frame[0], 3 * n_chans), BF16),
                pltpu.VMEM((frame[0], 3 * n_chans), BF16),
                pltpu.VMEM((2, n_taps, 9 * n_chans, n_chans), BF16),
                pltpu.VMEM((n_frames,) + frame, F32),
                pltpu.VMEM((2, 8, n_chans), F32),
                pltpu.VMEM((8, n_chans), F32),
                pltpu.VMEM((2, 8, LANES), F32),
                pltpu.VMEM((2, n_time, 8, LANES), F32),
                pltpu.SemaphoreType.DMA((4,)),
                pltpu.SemaphoreType.DMA((2, n_taps)),
                pltpu.SemaphoreType.DMA((2,)),
                pltpu.SemaphoreType.DMA((2, 2)),
                pltpu.SemaphoreType.DMA((2, n_time)),
                pltpu.SemaphoreType.DMA((2, n_time)),
                pltpu.SemaphoreType.DMA((2,)),
            ],
            compiler_params=pltpu.CompilerParams(collective_id=0, has_side_effects=True, vmem_limit_bytes=60 * 1024 * 1024),
            name="decoder_blocks",
        )(latent.reshape((n_frames,) + frame), conv_kernels.reshape(n_layers, n_taps, 9 * n_chans, n_chans),
          conv_biases.reshape(n_layers, 1, n_chans), gn_gammas.reshape(n_layers, n_blk, LANES),
          gn_betas.reshape(n_layers, n_blk, LANES))
        return decoded.reshape(latent.shape)

    return jax.shard_map(local_fn, mesh=mesh, in_specs=(frame_spec, P(), P(), P(), P()), out_specs=frame_spec, check_vma=False)
```

time: 316 us -> 108 us (0.34)
  the two profiles are of different devices: /device:TPU:150 before, /device:TPU:21 now
where the time goes in v1:
time: 108 us
  Pallas kernels  102 us (94%)
  local copies, waits for them, and re-layouts  6.26 us (6%)
    pallas_call x1, Pallas kernels, local_fn(): pl.pallas_call(functools.partial(_kernel, n_time, n_layers, n_rows, n_col...  102 us
    unnamed x1, local copies, waits for them, and re-layouts  2.36 us

profile of v1, /device:TPU:21, one launch (start us, length us, event | category | flops | bytes accessed | tf_op | source)
XLA Modules:
  0.0 108.0 jit_solution(16648904707750494905)
XLA Ops:
  0.0 1.3 %reshape.20.bias_ref = f32[4,1,512]{2,1,0:T(1,128)} reshape(f32[4,512]{1,0:T(4,128)} %param.7) | data formatting | bytes 16384 | tf_op jit(solution)/shard_map/reshape | solution.py:311
  1.3 1.3 %reshape.21.gamma_ref = f32[4,4,128]{2,1,0:T(4,128)} reshape(f32[4,512]{1,0:T(4,128)} %param.8) | data formatting | bytes 16384 | tf_op jit(solution)/shard_map/reshape | solution.py:311
  2.6 1.3 %reshape.22.beta_ref = f32[4,4,128]{2,1,0:T(4,128)} reshape(f32[4,512]{1,0:T(4,128)} %param.9) | data formatting | bytes 16384 | tf_op jit(solution)/shard_map/reshape | solution.py:312
  3.9 101.8 %decoder_blocks.1 = bf16[2,576,512]{2,1,0:T(8,128)(2,1)} custom-call(bf16[2,576,512]{2,1,0:T(8,128)(2,1)} %bitcast.5, bf16[4,3,4608,512]{3,2,1,0:T(8,128)(2,1)} %bitcast.3, f32[4,1,512]{2,1,0:T(1,128)} %reshape.20.bias_ref, f32[4,4,128]{2,1,0:T(4,128)} %reshape.21.gamma_ref, f32[4,4,128]{2,1,0:T(4,128)} %reshape.22.beta_ref), custom_call_target="tpu_custom_call" | custom-call | tf_op jit(solution)/shard_map/decoder_blocks/pallas_call | solution.py:282
  105.7 2.4 %copy.7 = bf16[2,6,96,512]{3,2,1,0:T(8,128)(2,1)} copy(bf16[2,6,96,512]{3,2,1,0:T(8,128)(2,1)} %bitcast.4) | data formatting | bytes 2359296

commit v2 on v1

--- a/solution.py
+++ b/solution.py
@@ -17,9 +17,9 @@
 
 
 def _kernel(n_time, n_layers, n_rows, n_cols, n_chans, elem_count,
-            x_hbm, w_hbm, bias_ref, gamma_ref, beta_ref, out_hbm,
+            x_hbm, w_hbm, bias_hbm, gamma_hbm, beta_hbm, out_hbm,
             raw, xres, act_h0, act_h1, act_a0, act_a1, wbuf, accs, st, ss, stat_tx, stat_rx,
-            x_sems, w_sems, halo_send, halo_recv, stat_send, stat_recv, out_sems):
+            params_in, bias_ref, gamma_ref, beta_ref, x_sems, p_sems, w_sems, halo_send, halo_recv, stat_send, stat_recv, out_sems):
     dp = lax.axis_index("dp")
     me = lax.axis_index("cp")
     acts = (act_h0, act_h1, act_a0, act_a1)
@@ -66,8 +66,6 @@
     def finish_stats(layer, parity):
         for dist in range(1, n_time):
             stat_arrival(parity, dist).wait_recv()
-        for dist in range(1, n_time):
-            stat_copy(parity, dist).wait_send()
         total = stat_rx[parity, 0]
         for src in range(1, n_time):
             total = total + stat_rx[parity, src]
@@ -79,11 +77,12 @@
             step *= 2
         mean = total[:n_blk] / elem_count
         var = total[n_blk:] / elem_count - mean * mean
-        scale = lax.rsqrt(var + NORM_EPS) * gamma_ref[layer]
-        shift = beta_ref[layer] - mean * scale
+        rstd = lax.rsqrt(var + NORM_EPS)
         for blk in range(n_blk):
-            ss[0:1, blk * LANES:(blk + 1) * LANES] = scale[blk:blk + 1]
-            ss[1:2, blk * LANES:(blk + 1) * LANES] = shift[blk:blk + 1]
+            lanes = slice(blk * LANES, (blk + 1) * LANES)
+            scale = rstd[blk:blk + 1] * gamma_ref[layer, :, lanes]
+            ss[0:1, lanes] = scale
+            ss[1:2, lanes] = beta_ref[layer, :, lanes] - mean[blk:blk + 1] * scale
 
     def add_stats(val, lanes):
         grouped = val.reshape(val.shape[0] // 8, 8, val.shape[1])
@@ -110,7 +109,7 @@
         def pop_item(layer, odd, t, row, q):
             rows = slice(row * n_cols, (row + 1) * n_cols)
             lanes = slice(q * TILE, (q + 1) * TILE)
-            val = accs[t, rows, lanes] + bias_ref[layer, 0:1, lanes]
+            val = accs[t, rows, lanes] + bias_ref[layer, :, lanes]
             val = val.astype(BF16).astype(F32)
             val = val + xres[0, t, rows, lanes].astype(F32) * odd.astype(F32)
             val = val.astype(BF16)
@@ -118,29 +117,49 @@
             xres[1 - odd, t, rows, lanes] = val
             add_stats(val.astype(F32), lanes)
 
-        def group(parity, k, act, t, rows, first, items):
+        def products(parity, steps, rows, items, parts=None):
             lo, hi = rows[0], rows[-1] + 1
             done = 0
-            parts = {}
-            for idx, di in enumerate((0, -1, 1)):
+            parts = dict(parts or {})
+            for idx, (k, act, di, chan, width) in enumerate(steps):
                 r0, r1 = max(lo, -di), min(hi, n_rows - di)
-                weight = wbuf[parity, k, (di + 1) * 3 * n_chans:(di + 2) * 3 * n_chans, :]
-                prod = jnp.dot(act[(r0 + di) * n_cols:(r1 + di) * n_cols, :], weight, preferred_element_type=F32)
+                rows_in = slice((r0 + di) * n_cols, (r1 + di) * n_cols)
+                base = (di + 1) * 3 * n_chans
+                prod = None
+                if width == n_chans:
+                    prod = jnp.dot(act[rows_in, :], wbuf[parity, k, base:base + 3 * n_chans, :], preferred_element_type=F32)
+                else:
+                    for dj in range(3):
+                        at = dj * n_chans + chan
+                        term = jnp.dot(act[rows_in, at:at + width], wbuf[parity, k, base + at:base + at + width, :],
+                                       preferred_element_type=F32)
+                        prod = term if prod is None else prod + term
                 for row in range(r0, r1):
                     piece = prod[(row - r0) * n_cols:(row - r0 + 1) * n_cols]
                     parts[row] = piece if row not in parts else parts[row] + piece
-                upto = (len(items) * (idx + 1)) // 3
+                upto = (len(items) * (idx + 1)) // len(steps)
                 for item in items[done:upto]:
                     item()
                 done = upto
-            for row in range(lo, hi):
-                here = slice(row * n_cols, (row + 1) * n_cols)
-                if first:
-                    accs[t, here, :] = parts[row]
-                else:
-                    accs[t, here, :] += parts[row]
+            return parts
+
+        def tap(k, act, row_taps=(0, -1, 1)):
+            return [(k, act, di, 0, n_chans) for di in row_taps]
+
+        def tap_halves(k, act):
+            return [(k, act, di, chan, n_chans // 2) for chan in (0, n_chans // 2) for di in (0, -1, 1)]
+
+        def put(t, parts):
+            for row, part in parts.items():
+                accs[t, row * n_cols:(row + 1) * n_cols, :] = part
+
+        def add(t, parts):
+            for row, part in parts.items():
+                accs[t, row * n_cols:(row + 1) * n_cols, :] += part
 
         whole = range(n_rows)
+        top = range(half_rows)
+        low = range(half_rows, n_rows)
 
         def pops(layer, odd, t, rows):
             return [functools.partial(pop_item, layer, odd, t, row, q) for row in rows for q in range(n_half)]
@@ -150,6 +169,10 @@
             pl.semaphore_signal(barrier, inc=1, device_id=(dp, peer(dist)), device_id_type=MESH)
         for t in (1, 0):
             pltpu.make_async_copy(x_hbm.at[t], raw.at[t], x_sems.at[t]).start()
+        params = [pltpu.make_async_copy(src, params_in.at[i], p_sems.at[i])
+                  for i, src in enumerate((bias_hbm, gamma_hbm, beta_hbm))]
+        for copy in params:
+            copy.start()
         for k in (2, 1, 0):
             weight_copy(0, 0, k).start()
         for t in (1, 0):
@@ -171,8 +194,12 @@
 
         @pl.when(has_next)
         def _():
-            for t in (1, 0):
-                halo_copy(x_hbm.at[t], 0, t).start()
+            halo_copy(raw.at[1], 0, 1).start()
+
+        for i, (copy, dst) in enumerate(zip(params, (bias_ref, gamma_ref, beta_ref))):
+            copy.wait()
+            for layer in range(n_layers):
+                dst[layer] = params_in[i, layer:layer + 1, :]
 
         def layer_step(layer, carry):
             parity = lax.rem(layer, 2)
@@ -186,17 +213,22 @@
                     weight_copy(layer + 1, nxt, k).start()
 
             finish_stats(layer, parity)
+
+            @pl.when(has_next)
+            def _():
+                halo_copy(raw.at[0], parity, 0).start()
+
             st[...] = jnp.zeros_like(st)
-            first_half = range(n_blk // 2)
-            second_half = range(n_blk // 2, n_blk)
-            for item in norm_items(1, act_a1, first_half):
+            early = range(n_blk // 2)
+            late = range(n_blk // 2, n_blk)
+            for item in norm_items(1, act_a1, early):
                 item()
             weight_copy(layer, parity, 2).wait()
-            for item in norm_items(1, act_a1, second_half):
-                item()
-            group(parity, 2, act_a1, 1, whole, True, norm_items(0, act_a0, range(n_blk)))
-
+            steps = tap_halves(2, act_a1)
+            parts = products(parity, steps[:3], whole, norm_items(1, act_a1, late))
+            put(1, products(parity, steps[3:], whole, norm_items(0, act_a0, range(n_blk)), parts))
             weight_copy(layer, parity, 1).wait()
+            weight_copy(layer, parity, 0).wait()
 
             @pl.when(has_prev)
             def _():
@@ -204,10 +236,8 @@
 
             src1 = jnp.where(has_prev, 3 + 2 * parity, 0)
             src0 = jnp.where(has_prev, 2 + 2 * parity, 0)
-            group(parity, 1, act_a0, 1, whole, False, norm_items(src1, act_h1, range(n_blk)))
-
-            weight_copy(layer, parity, 0).wait()
-
+            parts = products(parity, tap(1, act_a0), whole, norm_items(src1, act_h1, range(n_blk)))
+            add(1, products(parity, tap(0, act_h1), whole, [], parts))
             @pl.when(has_next)
             def _():
                 halo_copy(raw.at[1], nxt, 1).wait_send()
@@ -217,41 +247,36 @@
                 for t in (1, 0):
                     pltpu.make_async_copy(x_hbm.at[t], xres.at[0, t], x_sems.at[2 + t]).wait()
 
-            group(parity, 0, act_h1, 1, whole, False, [])
-
+            put(0, products(parity, tap(2, act_a0, (0,)), whole, pops(layer, odd, 1, whole)))
+            @pl.when(jnp.logical_and(more, has_next))
+            def _():
+                halo_copy(raw.at[1], nxt, 1).start()
+
+            @pl.when(jnp.logical_not(more))
+            def _():
+                pltpu.make_async_copy(raw.at[1], out_hbm.at[1], out_sems.at[1]).start()
+
+            for dist in range(1, n_time):
+                stat_copy(parity, dist).wait_send()
+
+            add(0, products(parity, tap(2, act_a0, (-1, 1)), whole, []))
             @pl.when(has_prev)
             def _():
                 halo_copy(raw.at[0], parity, 0).wait_recv()
 
-            for item in pops(layer, odd, 1, whole):
+            @pl.when(has_next)
+            def _():
+                halo_copy(raw.at[0], nxt, 0).wait_send()
+
+            add(0, products(parity, tap(1, act_h1), whole, norm_items(src0, act_h0, range(n_blk))))
+            add(0, products(parity, tap(0, act_h0), top, []))
+            add(0, products(parity, tap(0, act_h0), low, pops(layer, odd, 0, top)))
+            for item in pops(layer, odd, 0, low):
                 item()
 
-            @pl.when(jnp.logical_and(more, has_next))
-            def _():
-                halo_copy(raw.at[1], nxt, 1).start()
-
-            @pl.when(jnp.logical_not(more))
-            def _():
-                pltpu.make_async_copy(raw.at[1], out_hbm.at[1], out_sems.at[1]).start()
-
-            group(parity, 2, act_a0, 0, whole, True, norm_items(src0, act_h0, range(n_blk)))
-            group(parity, 1, act_h1, 0, whole, False, [])
-
-            @pl.when(has_next)
-            def _():
-                halo_copy(raw.at[0], nxt, 0).wait_send()
-
-            group(parity, 0, act_h0, 0, whole, False, [])
-            for item in pops(layer, odd, 0, whole):
-                item()
-
             @pl.when(more)
             def _():
                 send_stats(nxt)
-
-            @pl.when(jnp.logical_and(more, has_next))
-            def _():
-                halo_copy(raw.at[0], nxt, 0).start()
 
             @pl.when(jnp.logical_not(more))
             def _():
@@ -274,15 +299,13 @@
         n_frames, n_rows, n_cols, n_chans = latent.shape
         n_layers = conv_kernels.shape[0]
         n_taps = conv_kernels.shape[1]
-        n_blk = n_chans // LANES
         elem_count = n_time * n_frames * n_rows * n_cols * (n_chans // GROUPS)
         frame = (n_rows * n_cols, n_chans)
         any_spec = pl.BlockSpec(memory_space=pl.ANY)
-        vmem_spec = pl.BlockSpec(memory_space=pltpu.VMEM)
         decoded = pl.pallas_call(
             functools.partial(_kernel, n_time, n_layers, n_rows, n_cols, n_chans, float(elem_count)),
             out_shape=jax.ShapeDtypeStruct((n_frames,) + frame, BF16),
-            in_specs=[any_spec, any_spec, vmem_spec, vmem_spec, vmem_spec],
+            in_specs=[any_spec] * 5,
             out_specs=any_spec,
             scratch_shapes=[
                 pltpu.VMEM((6,) + frame, BF16),
@@ -297,7 +320,12 @@
                 pltpu.VMEM((8, n_chans), F32),
                 pltpu.VMEM((2, 8, LANES), F32),
                 pltpu.VMEM((2, n_time, 8, LANES), F32),
+                pltpu.VMEM((3, n_layers, n_chans), F32),
+                pltpu.VMEM((n_layers, 1, n_chans), F32),
+                pltpu.VMEM((n_layers, 1, n_chans), F32),
+                pltpu.VMEM((n_layers, 1, n_chans), F32),
                 pltpu.SemaphoreType.DMA((4,)),
+                pltpu.SemaphoreType.DMA((3,)),
                 pltpu.SemaphoreType.DMA((2, n_taps)),
                 pltpu.SemaphoreType.DMA((2,)),
                 pltpu.SemaphoreType.DMA((2, 2)),
@@ -308,8 +336,7 @@
             compiler_params=pltpu.CompilerParams(collective_id=0, has_side_effects=True, vmem_limit_bytes=60 * 1024 * 1024),
             name="decoder_blocks",
         )(latent.reshape((n_frames,) + frame), conv_kernels.reshape(n_layers, n_taps, 9 * n_chans, n_chans),
-          conv_biases.reshape(n_layers, 1, n_chans), gn_gammas.reshape(n_layers, n_blk, LANES),
-          gn_betas.reshape(n_layers, n_blk, LANES))
+          conv_biases, gn_gammas, gn_betas)
         return decoded.reshape(latent.shape)
 
     return jax.shard_map(local_fn, mesh=mesh, in_specs=(frame_spec, P(), P(), P(), P()), out_specs=frame_spec, check_vma=False)

time: 108 us -> 101 us (0.935)
  local copies, waits for them, and re-layouts: 6.26 us -> 2.36 us
  Pallas kernels: 102 us -> 99 us
    reshape x3 -> x0, local copies, waits for them, and re-layouts: 3.9 us -> none  [the longest x1 1.3 us: local_fn(): gn_betas.reshape(n_layers, n_blk, LANES)]
    pallas_call x1, Pallas kernels: 102 us -> 99 us  [local_fn(): pl.pallas_call(functools.partial(_kernel, n_time, n_layers, n_rows, n_col...]
where the time goes in v2:
time: 101 us
  Pallas kernels  99 us (98%)
  local copies, waits for them, and re-layouts  2.36 us (2%)
    pallas_call x1, Pallas kernels, local_fn(): pl.pallas_call(functools.partial(_kernel, n_time, n_layers, n_rows, n_col...  99 us
    unnamed x1, local copies, waits for them, and re-layouts  2.36 us

profile of v2, /device:TPU:21, one launch (start us, length us, event | category | flops | bytes accessed | tf_op | source)
XLA Modules:
  0.0 101.4 jit_solution(14173644300494392390)
XLA Ops:
  0.0 99.0 %decoder_blocks.1 = bf16[2,576,512]{2,1,0:T(8,128)(2,1)} custom-call(bf16[2,576,512]{2,1,0:T(8,128)(2,1)} %bitcast.5, bf16[4,3,4608,512]{3,2,1,0:T(8,128)(2,1)} %bitcast.3, f32[4,512]{1,0:T(4,128)} %bias_hbm.1, f32[4,512]{1,0:T(4,128)} %gamma_hbm.1, f32[4,512]{1,0:T(4,128)} %beta_hbm.1), custom_call_target="tpu_custom_call" | custom-call | tf_op jit(solution)/shard_map/decoder_blocks/pallas_call | solution.py:305
  99.0 2.4 %copy.7 = bf16[2,6,96,512]{3,2,1,0:T(8,128)(2,1)} copy(bf16[2,6,96,512]{3,2,1,0:T(8,128)(2,1)} %bitcast.4) | data formatting | bytes 2359296

commit v3 on v2

v3 whole, which is shorter than its diff:
```python
import functools

import jax
import jax.numpy as jnp
from jax import lax
from jax.experimental import pallas as pl
from jax.experimental.pallas import tpu as pltpu
from jax.sharding import PartitionSpec as P

GROUPS = 32
NORM_EPS = 1e-6
F32 = jnp.float32
BF16 = jnp.bfloat16
MESH = pl.DeviceIdType.MESH
TILE = 256
LANES = 128


def _kernel(n_time, n_layers, n_rows, n_cols, n_chans, elem_count,
            x_hbm, w_hbm, bias_hbm, gamma_hbm, beta_hbm, own,
            halo, xres, act_h0, act_h1, act_a0, act_a1, wbuf, st, ss, stat_tx, stat_rx,
            params_in, bias_ref, gamma_ref, beta_ref, x_sems, p_sems, w_sems, halo_send, halo_recv, stat_send, stat_recv):
    dp = lax.axis_index("dp")
    me = lax.axis_index("cp")
    acts = (act_h0, act_h1, act_a0, act_a1)
    n_blk = n_chans // LANES
    n_half = n_chans // TILE
    frame_rows = n_rows * n_cols
    group_width = n_chans // GROUPS
    has_next = me < n_time - 1
    has_prev = me > 0
    half_rows = n_rows // 2
    n_pieces = 3

    def peer(dist):
        return lax.rem(me + dist, n_time)

    def halo_copies(parity, t):
        pieces = n_pieces if t == 1 else 1
        span = frame_rows // pieces
        return [pltpu.make_async_remote_copy(
            src_ref=own.at[t, i * span:(i + 1) * span], dst_ref=halo.at[2 * parity + t, i * span:(i + 1) * span],
            send_sem=halo_send.at[t, i], recv_sem=halo_recv.at[parity, t, i],
            device_id=(dp, lax.rem(me + 1, n_time)), device_id_type=MESH) for i in range(pieces)]

    def start_halo(cond, parity, t):
        @pl.when(cond)
        def _():
            for copy in halo_copies(parity, t):
                copy.start()

    def sent_halo(parity, t):
        @pl.when(has_next)
        def _():
            for copy in halo_copies(parity, t):
                copy.wait_send()

    def take_halo(parity, t, i):
        @pl.when(has_prev)
        def _():
            halo_copies(parity, t)[i].wait_recv()

    def weight_copy(layer, parity, k):
        return pltpu.make_async_copy(w_hbm.at[layer, k], wbuf.at[parity, k], w_sems.at[parity, k])

    def stat_copy(parity, dist):
        return pltpu.make_async_remote_copy(
            src_ref=stat_tx.at[parity], dst_ref=stat_rx.at[parity, me], send_sem=stat_send.at[parity, dist],
            recv_sem=stat_recv.at[parity], device_id=(dp, peer(dist)), device_id_type=MESH)

    def stat_arrivals(parity):
        return pltpu.make_async_copy(stat_rx.at[parity, 0:n_time - 1], stat_rx.at[parity, 0:n_time - 1], stat_recv.at[parity])

    far_first = sorted(range(1, n_time), key=lambda d: -min(d, n_time - d))

    def send_stats(parity):
        for row in range(2):
            total = jnp.sum(st[row], axis=0, keepdims=True)
            for blk in range(n_blk):
                stat_tx[parity, row * n_blk + blk:row * n_blk + blk + 1, :] = total[:, blk * LANES:(blk + 1) * LANES]
        stat_rx[parity, me] = stat_tx[parity]
        for dist in far_first:
            stat_copy(parity, dist).start()

    def finish_stats(layer, parity):
        stat_arrivals(parity).wait()
        total = stat_rx[parity, 0]
        for src in range(1, n_time):
            total = total + stat_rx[parity, src]
        lane = lax.broadcasted_iota(jnp.int32, total.shape, 1)
        step = 1
        while step < group_width:
            other = jnp.where((lane & step) != 0, pltpu.roll(total, step, 1), pltpu.roll(total, LANES - step, 1))
            total = total + other
            step *= 2
        mean = total[:n_blk] / elem_count
        var = total[n_blk:] / elem_count - mean * mean
        rstd = lax.rsqrt(var + NORM_EPS)
        for blk in range(n_blk):
            lanes = slice(blk * LANES, (blk + 1) * LANES)
            scale = rstd[blk:blk + 1] * gamma_ref[layer, :, lanes]
            ss[0:1, lanes] = scale
            ss[1:2, lanes] = beta_ref[layer, :, lanes] - mean[blk:blk + 1] * scale

    def add_stats(val, lanes):
        grouped = val.reshape(val.shape[0] // 8, 8, val.shape[1])
        st[0, :, lanes] += jnp.sum(grouped, axis=0)
        st[1, :, lanes] += jnp.sum(grouped * grouped, axis=0)

    def norm_item(source, act, row, blk):
        rows = slice(row * n_cols, (row + 1) * n_cols)
        lanes = slice(blk * LANES, (blk + 1) * LANES)
        val = source(rows, lanes)
        val = (val * ss[0:1, lanes] + ss[1:2, lanes]).astype(BF16).astype(F32)
        val = val * lax.logistic(val)
        col = lax.broadcasted_iota(jnp.int32, val.shape, 0)
        act[rows, n_chans + blk * LANES:n_chans + (blk + 1) * LANES] = val.astype(BF16)
        before = jnp.where(col == 0, 0.0, pltpu.roll(val, 1, 0))
        act[rows, blk * LANES:(blk + 1) * LANES] = before.astype(BF16)
        after = jnp.where(col == n_cols - 1, 0.0, pltpu.roll(val, n_cols - 1, 0))
        act[rows, 2 * n_chans + blk * LANES:2 * n_chans + (blk + 1) * LANES] = after.astype(BF16)

    def norm_items(source, act, blks, rows=None):
        return [functools.partial(norm_item, source, act, row, blk) for row in (rows or range(n_rows)) for blk in blks]

    def own_frame(t):
        return lambda rows, lanes: own[t, rows, lanes].astype(F32)

    def halo_frame(parity, t):
        return lambda rows, lanes: jnp.where(has_prev, halo[2 * parity + t, rows, lanes].astype(F32), own[0, rows, lanes].astype(F32))

    def run_body():
        def finish_item(layer, odd, keep, t, row, q, part):
            rows = slice(row * n_cols, (row + 1) * n_cols)
            lanes = slice(q * TILE, (q + 1) * TILE)
            val = part[:, lanes] + bias_ref[layer, :, lanes]
            val = val.astype(BF16).astype(F32)
            old = xres[t, rows, lanes].astype(F32)
            val = (val + old * keep).astype(BF16)
            own[t, rows, lanes] = val
            val = val.astype(F32)
            xres[t, rows, lanes] = jnp.where(odd == 1, val, old).astype(BF16)
            add_stats(val, lanes)

        def products(parity, steps, rows, items, parts=None):
            lo, hi = rows[0], rows[-1] + 1
            done = 0
            parts = dict(parts or {})
            for idx, (k, act, di, chan, width) in enumerate(steps):
                r0, r1 = max(lo, -di), min(hi, n_rows - di)
                rows_in = slice((r0 + di) * n_cols, (r1 + di) * n_cols)
                base = (di + 1) * 3 * n_chans
                prod = None
                if width == n_chans:
                    prod = jnp.dot(act[rows_in, :], wbuf[parity, k, base:base + 3 * n_chans, :], preferred_element_type=F32)
                else:
                    for dj in range(3):
                        at = dj * n_chans + chan
                        term = jnp.dot(act[rows_in, at:at + width], wbuf[parity, k, base + at:base + at + width, :],
                                       preferred_element_type=F32)
                        prod = term if prod is None else prod + term
                for row in range(r0, r1):
                    piece = prod[(row - r0) * n_cols:(row - r0 + 1) * n_cols]
                    parts[row] = piece if row not in parts else parts[row] + piece
                upto = (len(items) * (idx + 1)) // len(steps)
                for item in items[done:upto]:
                    item()
                done = upto
            return parts

        def tap(k, act, row_taps=(0, -1, 1)):
            return [(k, act, di, 0, n_chans) for di in row_taps]

        def tap_halves(k, act):
            return [(k, act, di, chan, n_chans // 2) for chan in (0, n_chans // 2) for di in (0, -1, 1)]

        whole = range(n_rows)
        top = range(half_rows)
        low = range(half_rows, n_rows)

        def finish(layer, odd, keep, t, parts, rows):
            return [functools.partial(finish_item, layer, odd, keep, t, row, q, parts[row]) for row in rows for q in range(n_half)]

        barrier = pltpu.get_barrier_semaphore()
        for dist in range(1, n_time):
            pl.semaphore_signal(barrier, inc=1, device_id=(dp, peer(dist)), device_id_type=MESH)
        for t in (1, 0):
            pltpu.make_async_copy(x_hbm.at[t], own.at[t], x_sems.at[t]).start()
        params = [pltpu.make_async_copy(src, params_in.at[i], p_sems.at[i])
                  for i, src in enumerate((bias_hbm, gamma_hbm, beta_hbm))]
        for copy in params:
            copy.start()
        for k in (2, 1, 0):
            weight_copy(0, 0, k).start()
        for t in (1, 0):
            pltpu.make_async_copy(x_hbm.at[t], xres.at[t], x_sems.at[2 + t]).start()
        st[...] = jnp.zeros_like(st)
        for t in (1, 0):
            pltpu.make_async_copy(x_hbm.at[t], own.at[t], x_sems.at[t]).wait()

            def stat_rows(i, carry, t=t):
                base = pl.multiple_of(i * n_cols, n_cols)
                for q in range(n_half):
                    lanes = slice(q * TILE, (q + 1) * TILE)
                    add_stats(own[t, pl.ds(base, n_cols), lanes].astype(F32), lanes)
                return carry

            lax.fori_loop(0, n_rows, stat_rows, 0)
        pl.semaphore_wait(barrier, n_time - 1)
        send_stats(0)

        start_halo(has_next, 0, 1)

        for i, (copy, dst) in enumerate(zip(params, (bias_ref, gamma_ref, beta_ref))):
            copy.wait()
            for layer in range(n_layers):
                dst[layer] = params_in[i, layer:layer + 1, :]

        def layer_step(layer, carry):
            parity = lax.rem(layer, 2)
            odd = parity
            nxt = 1 - parity
            more = layer < n_layers - 1

            @pl.when(more)
            def _():
                for k in (2, 1, 0):
                    weight_copy(layer + 1, nxt, k).start()

            finish_stats(layer, parity)

            start_halo(jnp.logical_and(has_next, layer > 0), parity, 0)

            st[...] = jnp.zeros_like(st)
            keep = odd.astype(F32)
            early = range(n_blk // 2)
            late = range(n_blk // 2, n_blk)
            for item in norm_items(own_frame(1), act_a1, early):
                item()
            weight_copy(layer, parity, 2).wait()
            steps = tap_halves(2, act_a1)
            frame1 = products(parity, steps[:3], whole, norm_items(own_frame(1), act_a1, late))
            frame1 = products(parity, steps[3:], whole, norm_items(own_frame(0), act_a0, range(n_blk)), frame1)
            weight_copy(layer, parity, 1).wait()
            weight_copy(layer, parity, 0).wait()

            take_halo(parity, 1, 0)
            sent_halo(nxt, 1)
            start_halo(jnp.logical_and(has_next, layer == 0), parity, 0)

            @pl.when(layer == 0)
            def _():
                for t in (1, 0):
                    pltpu.make_async_copy(x_hbm.at[t], xres.at[t], x_sems.at[2 + t]).wait()

            for i, di in enumerate((0, -1, 1)):
                if i > 0:
                    take_halo(parity, 1, i)
                items = norm_items(halo_frame(parity, 1), act_h1, range(n_blk), range(2 * i, 2 * i + 2))
                frame1 = products(parity, tap(1, act_a0, (di,)), whole, items, frame1)
            frame1 = products(parity, tap(0, act_h1), top, [], frame1)
            frame1 = products(parity, tap(0, act_h1), low, finish(layer, odd, keep, 1, frame1, top), frame1)
            frame0 = products(parity, tap(2, act_a0, (0,)), whole, finish(layer, odd, keep, 1, frame1, low))
            start_halo(jnp.logical_and(more, has_next), nxt, 1)

            for dist in range(1, n_time):
                stat_copy(parity, dist).wait_send()

            frame0 = products(parity, tap(2, act_a0, (-1, 1)), whole, [], frame0)
            take_halo(parity, 0, 0)
            sent_halo(nxt, 0)

            frame0 = products(parity, tap(1, act_h1), whole, norm_items(halo_frame(parity, 0), act_h0, range(n_blk)), frame0)
            frame0 = products(parity, tap(0, act_h0), top, [], frame0)
            frame0 = products(parity, tap(0, act_h0), low, finish(layer, odd, keep, 0, frame0, top), frame0)
            for item in finish(layer, odd, keep, 0, frame0, low):
                item()

            @pl.when(more)
            def _():
                send_stats(nxt)

            return carry

        lax.fori_loop(0, n_layers, layer_step, 0)

    run_body()


def solution(mesh):
    n_time = mesh.shape["cp"]
    frame_spec = P(("dp", "cp"))

    def local_fn(latent, conv_kernels, conv_biases, gn_gammas, gn_betas):
        n_frames, n_rows, n_cols, n_chans = latent.shape
        n_layers = conv_kernels.shape[0]
        n_taps = conv_kernels.shape[1]
        elem_count = n_time * n_frames * n_rows * n_cols * (n_chans // GROUPS)
        frame = (n_rows * n_cols, n_chans)
        any_spec = pl.BlockSpec(memory_space=pl.ANY)
        decoded = pl.pallas_call(
            functools.partial(_kernel, n_time, n_layers, n_rows, n_cols, n_chans, float(elem_count)),
            out_shape=pltpu.VMEM((n_frames,) + frame, BF16),
            in_specs=[any_spec] * 5,
            out_specs=pl.BlockSpec(memory_space=pltpu.VMEM),
            scratch_shapes=[
                pltpu.VMEM((4,) + frame, BF16),
                pltpu.VMEM((n_frames,) + frame, BF16),
                pltpu.VMEM((frame[0], 3 * n_chans), BF16),
                pltpu.VMEM((frame[0], 3 * n_chans), BF16),
                pltpu.VMEM((frame[0], 3 * n_chans), BF16),
                pltpu.VMEM((frame[0], 3 * n_chans), BF16),
                pltpu.VMEM((2, n_taps, 9 * n_chans, n_chans), BF16),
                pltpu.VMEM((2, 8, n_chans), F32),
                pltpu.VMEM((8, n_chans), F32),
                pltpu.VMEM((2, 8, LANES), F32),
                pltpu.VMEM((2, n_time, 8, LANES), F32),
                pltpu.VMEM((3, n_layers, n_chans), F32),
                pltpu.VMEM((n_layers, 1, n_chans), F32),
                pltpu.VMEM((n_layers, 1, n_chans), F32),
                pltpu.VMEM((n_layers, 1, n_chans), F32),
                pltpu.SemaphoreType.DMA((4,)),
                pltpu.SemaphoreType.DMA((3,)),
                pltpu.SemaphoreType.DMA((2, n_taps)),
                pltpu.SemaphoreType.DMA((2, 3)),
                pltpu.SemaphoreType.DMA((2, 2, 3)),
                pltpu.SemaphoreType.DMA((2, n_time)),
                pltpu.SemaphoreType.DMA((2,)),
            ],
            compiler_params=pltpu.CompilerParams(collective_id=0, has_side_effects=True, vmem_limit_bytes=60 * 1024 * 1024),
            name="decoder_blocks",
        )(latent.reshape((n_frames,) + frame), conv_kernels.reshape(n_layers, n_taps, 9 * n_chans, n_chans),
          conv_biases, gn_gammas, gn_betas)
        return decoded.reshape(latent.shape)

    return jax.shard_map(local_fn, mesh=mesh, in_specs=(frame_spec, P(), P(), P(), P()), out_specs=frame_spec, check_vma=False)
```

time: 101 us -> 98.3 us (0.973)
  Pallas kernels: 99 us -> 97.1 us
  local copies, waits for them, and re-layouts: 2.36 us -> 1.02 us
    pallas_call x1, Pallas kernels: 99 us -> 97.1 us  [local_fn(): pl.pallas_call(functools.partial(_kernel, n_time, n_layers, n_rows, n_col...]
    unnamed x1, local copies, waits for them, and re-layouts: 2.36 us -> 1.02 us
where the time goes in v3:
time: 98.3 us; the launch traced here: 98.1 us
  Pallas kernels  97.1 us (99%)
  local copies, waits for them, and re-layouts  1.02 us (1%)
    pallas_call x1, Pallas kernels, local_fn(): pl.pallas_call(functools.partial(_kernel, n_time, n_layers, n_rows, n_col...  97.1 us

profile of v3, /device:TPU:21, one launch (start us, length us, event | category | flops | bytes accessed | tf_op | source)
XLA Modules:
  0.0 98.1 jit_solution(11800900593844256505)
XLA Ops:
  0.0 97.1 %decoder_blocks.1 = bf16[2,576,512]{2,1,0:T(8,128)(2,1)S(1)} custom-call(bf16[2,576,512]{2,1,0:T(8,128)(2,1)} %bitcast.5, bf16[4,3,4608,512]{3,2,1,0:T(8,128)(2,1)} %bitcast.4, f32[4,512]{1,0:T(4,128)} %bias_hbm.1, f32[4,512]{1,0:T(4,128)} %gamma_hbm.1, f32[4,512]{1,0:T(4,128)} %beta_hbm.1), custom_call_target="tpu_custom_call" | custom-call | tf_op jit(solution)/shard_map/decoder_blocks/pallas_call | solution.py:301
  97.1 1.0 %copy.7 = bf16[2,6,96,512]{3,2,1,0:T(8,128)(2,1)} copy(bf16[2,6,96,512]{3,2,1,0:T(8,128)(2,1)S(1)} %bitcast.3) | data formatting | bytes 2359296

commit v4 on v3

--- a/solution.py
+++ b/solution.py
@@ -68,6 +68,11 @@
             src_ref=stat_tx.at[parity], dst_ref=stat_rx.at[parity, me], send_sem=stat_send.at[parity, dist],
             recv_sem=stat_recv.at[parity], device_id=(dp, peer(dist)), device_id_type=MESH)
 
+    def tree_sum(terms):
+        while len(terms) > 1:
+            terms = [terms[i] + terms[i + 1] if i + 1 < len(terms) else terms[i] for i in range(0, len(terms), 2)]
+        return terms[0]
+
     def stat_arrivals(parity):
         return pltpu.make_async_copy(stat_rx.at[parity, 0:n_time - 1], stat_rx.at[parity, 0:n_time - 1], stat_recv.at[parity])
 
@@ -84,15 +89,14 @@
 
     def finish_stats(layer, parity):
         stat_arrivals(parity).wait()
-        total = stat_rx[parity, 0]
-        for src in range(1, n_time):
-            total = total + stat_rx[parity, src]
+        total = tree_sum([stat_rx[parity, src] for src in range(n_time)])
         lane = lax.broadcasted_iota(jnp.int32, total.shape, 1)
-        step = 1
-        while step < group_width:
-            other = jnp.where((lane & step) != 0, pltpu.roll(total, step, 1), pltpu.roll(total, LANES - step, 1))
-            total = total + other
-            step *= 2
+        place = lane & (group_width - 1)
+        terms = [total]
+        for shift in range(1, group_width):
+            terms.append(jnp.where(place >= shift, pltpu.roll(total, shift, 1), 0.0))
+            terms.append(jnp.where(place < group_width - shift, pltpu.roll(total, LANES - shift, 1), 0.0))
+        total = tree_sum(terms)
         mean = total[:n_blk] / elem_count
         var = total[n_blk:] / elem_count - mean * mean
         rstd = lax.rsqrt(var + NORM_EPS)
@@ -113,11 +117,13 @@
         val = source(rows, lanes)
         val = (val * ss[0:1, lanes] + ss[1:2, lanes]).astype(BF16).astype(F32)
         val = val * lax.logistic(val)
-        col = lax.broadcasted_iota(jnp.int32, val.shape, 0)
+        col = lax.broadcasted_iota(jnp.int32, (8, LANES), 0)
         act[rows, n_chans + blk * LANES:n_chans + (blk + 1) * LANES] = val.astype(BF16)
-        before = jnp.where(col == 0, 0.0, pltpu.roll(val, 1, 0))
+        before = pltpu.roll(val, 1, 0)
+        before = jnp.concatenate([jnp.where(col == 0, 0.0, before[:8]), before[8:]], axis=0)
         act[rows, blk * LANES:(blk + 1) * LANES] = before.astype(BF16)
-        after = jnp.where(col == n_cols - 1, 0.0, pltpu.roll(val, n_cols - 1, 0))
+        after = pltpu.roll(val, n_cols - 1, 0)
+        after = jnp.concatenate([after[:-8], jnp.where(col == 7, 0.0, after[-8:])], axis=0)
         act[rows, 2 * n_chans + blk * LANES:2 * n_chans + (blk + 1) * LANES] = after.astype(BF16)
 
     def norm_items(source, act, blks, rows=None):
@@ -130,17 +136,16 @@
         return lambda rows, lanes: jnp.where(has_prev, halo[2 * parity + t, rows, lanes].astype(F32), own[0, rows, lanes].astype(F32))
 
     def run_body():
-        def finish_item(layer, odd, keep, t, row, q, part):
+        def finish_item(layer, odd, t, row, q, part):
             rows = slice(row * n_cols, (row + 1) * n_cols)
             lanes = slice(q * TILE, (q + 1) * TILE)
             val = part[:, lanes] + bias_ref[layer, :, lanes]
-            val = val.astype(BF16).astype(F32)
-            old = xres[t, rows, lanes].astype(F32)
-            val = (val + old * keep).astype(BF16)
+            val = val.astype(BF16)
+            if odd:
+                val = (val.astype(F32) + xres[t, rows, lanes].astype(F32)).astype(BF16)
+                xres[t, rows, lanes] = val
             own[t, rows, lanes] = val
-            val = val.astype(F32)
-            xres[t, rows, lanes] = jnp.where(odd == 1, val, old).astype(BF16)
-            add_stats(val, lanes)
+            add_stats(val.astype(F32), lanes)
 
         def products(parity, steps, rows, items, parts=None):
             lo, hi = rows[0], rows[-1] + 1
@@ -178,11 +183,11 @@
         top = range(half_rows)
         low = range(half_rows, n_rows)
 
-        def finish(layer, odd, keep, t, parts, rows):
-            return [functools.partial(finish_item, layer, odd, keep, t, row, q, parts[row]) for row in rows for q in range(n_half)]
+        def finish(layer, odd, t, parts, rows):
+            return [functools.partial(finish_item, layer, odd, t, row, q, parts[row]) for row in rows for q in range(n_half)]
 
         barrier = pltpu.get_barrier_semaphore()
-        for dist in range(1, n_time):
+        for dist in far_first:
             pl.semaphore_signal(barrier, inc=1, device_id=(dp, peer(dist)), device_id_type=MESH)
         for t in (1, 0):
             pltpu.make_async_copy(x_hbm.at[t], own.at[t], x_sems.at[t]).start()
@@ -216,9 +221,8 @@
             for layer in range(n_layers):
                 dst[layer] = params_in[i, layer:layer + 1, :]
 
-        def layer_step(layer, carry):
-            parity = lax.rem(layer, 2)
-            odd = parity
+        def layer_step(layer, parity):
+            odd = parity == 1
             nxt = 1 - parity
             more = layer < n_layers - 1
 
@@ -232,7 +236,6 @@
             start_halo(jnp.logical_and(has_next, layer > 0), parity, 0)
 
             st[...] = jnp.zeros_like(st)
-            keep = odd.astype(F32)
             early = range(n_blk // 2)
             late = range(n_blk // 2, n_blk)
             for item in norm_items(own_frame(1), act_a1, early):
@@ -245,7 +248,6 @@
             weight_copy(layer, parity, 0).wait()
 
             take_halo(parity, 1, 0)
-            sent_halo(nxt, 1)
             start_halo(jnp.logical_and(has_next, layer == 0), parity, 0)
 
             @pl.when(layer == 0)
@@ -259,8 +261,9 @@
                 items = norm_items(halo_frame(parity, 1), act_h1, range(n_blk), range(2 * i, 2 * i + 2))
                 frame1 = products(parity, tap(1, act_a0, (di,)), whole, items, frame1)
             frame1 = products(parity, tap(0, act_h1), top, [], frame1)
-            frame1 = products(parity, tap(0, act_h1), low, finish(layer, odd, keep, 1, frame1, top), frame1)
-            frame0 = products(parity, tap(2, act_a0, (0,)), whole, finish(layer, odd, keep, 1, frame1, low))
+            sent_halo(nxt, 1)
+            frame1 = products(parity, tap(0, act_h1), low, finish(layer, odd, 1, frame1, top), frame1)
+            frame0 = products(parity, tap(2, act_a0, (0,)), whole, finish(layer, odd, 1, frame1, low))
             start_halo(jnp.logical_and(more, has_next), nxt, 1)
 
             for dist in range(1, n_time):
@@ -272,17 +275,20 @@
 
             frame0 = products(parity, tap(1, act_h1), whole, norm_items(halo_frame(parity, 0), act_h0, range(n_blk)), frame0)
             frame0 = products(parity, tap(0, act_h0), top, [], frame0)
-            frame0 = products(parity, tap(0, act_h0), low, finish(layer, odd, keep, 0, frame0, top), frame0)
-            for item in finish(layer, odd, keep, 0, frame0, low):
+            frame0 = products(parity, tap(0, act_h0), low, finish(layer, odd, 0, frame0, top), frame0)
+            for item in finish(layer, odd, 0, frame0, low):
                 item()
 
             @pl.when(more)
             def _():
                 send_stats(nxt)
 
+        def block_step(block, carry):
+            for parity in range(2):
+                layer_step(2 * block + parity, parity)
             return carry
 
-        lax.fori_loop(0, n_layers, layer_step, 0)
+        lax.fori_loop(0, n_layers // 2, block_step, 0)
 
     run_body()
 

time: 98.3 us -> 96.2 us (0.979)
  Pallas kernels: 97.1 us -> 95.1 us
    pallas_call x1, Pallas kernels: 97.1 us -> 95.1 us  [local_fn(): pl.pallas_call(functools.partial(_kernel, n_time, n_layers, n_rows, n_col...]
where the time goes in v4:
time: 96.2 us; the launch traced here: 96.1 us
  Pallas kernels  95.1 us (99%)
  local copies, waits for them, and re-layouts  1.02 us (1%)
    pallas_call x1, Pallas kernels, local_fn(): pl.pallas_call(functools.partial(_kernel, n_time, n_layers, n_rows, n_col...  95.1 us

profile of v4, /device:TPU:21, one launch (start us, length us, event | category | flops | bytes accessed | tf_op | source)
XLA Modules:
  0.0 96.1 jit_solution(8752506602619108921)
XLA Ops:
  0.0 95.1 %decoder_blocks.1 = bf16[2,576,512]{2,1,0:T(8,128)(2,1)S(1)} custom-call(bf16[2,576,512]{2,1,0:T(8,128)(2,1)} %bitcast.5, bf16[4,3,4608,512]{3,2,1,0:T(8,128)(2,1)} %bitcast.4, f32[4,512]{1,0:T(4,128)} %bias_hbm.1, f32[4,512]{1,0:T(4,128)} %gamma_hbm.1, f32[4,512]{1,0:T(4,128)} %beta_hbm.1), custom_call_target="tpu_custom_call" | custom-call | tf_op jit(solution)/shard_map/decoder_blocks/pallas_call | solution.py:307
  95.1 1.0 %copy.7 = bf16[2,6,96,512]{3,2,1,0:T(8,128)(2,1)} copy(bf16[2,6,96,512]{3,2,1,0:T(8,128)(2,1)S(1)} %bitcast.3) | data formatting | bytes 2359296

commit v5 on v4

--- a/solution.py
+++ b/solution.py
@@ -232,6 +232,8 @@
                     weight_copy(layer + 1, nxt, k).start()
 
             finish_stats(layer, parity)
+            for dist in range(1, n_time):
+                stat_copy(parity, dist).wait_send()
 
             start_halo(jnp.logical_and(has_next, layer > 0), parity, 0)
 
@@ -260,14 +262,10 @@
                     take_halo(parity, 1, i)
                 items = norm_items(halo_frame(parity, 1), act_h1, range(n_blk), range(2 * i, 2 * i + 2))
                 frame1 = products(parity, tap(1, act_a0, (di,)), whole, items, frame1)
-            frame1 = products(parity, tap(0, act_h1), top, [], frame1)
+            frame1 = products(parity, tap(0, act_h1), whole, [], frame1)
             sent_halo(nxt, 1)
-            frame1 = products(parity, tap(0, act_h1), low, finish(layer, odd, 1, frame1, top), frame1)
-            frame0 = products(parity, tap(2, act_a0, (0,)), whole, finish(layer, odd, 1, frame1, low))
+            frame0 = products(parity, tap(2, act_a0, (0,)), whole, finish(layer, odd, 1, frame1, whole))
             start_halo(jnp.logical_and(more, has_next), nxt, 1)
-
-            for dist in range(1, n_time):
-                stat_copy(parity, dist).wait_send()
 
             frame0 = products(parity, tap(2, act_a0, (-1, 1)), whole, [], frame0)
             take_halo(parity, 0, 0)

time: 96.2 us -> 96 us (level)
  no operation moved by 1% of the time
where the time goes in v5:
time: 96 us; the launch traced here: 95.8 us
  Pallas kernels  94.8 us (99%)
  local copies, waits for them, and re-layouts  1.02 us (1%)
    pallas_call x1, Pallas kernels, local_fn(): pl.pallas_call(functools.partial(_kernel, n_time, n_layers, n_rows, n_col...  94.8 us

profile of v5, /device:TPU:21, one launch (start us, length us, event | category | flops | bytes accessed | tf_op | source)
XLA Modules:
  0.0 95.8 jit_solution(12734576838847695316)
XLA Ops:
  0.0 94.8 %decoder_blocks.1 = bf16[2,576,512]{2,1,0:T(8,128)(2,1)S(1)} custom-call(bf16[2,576,512]{2,1,0:T(8,128)(2,1)} %bitcast.5, bf16[4,3,4608,512]{3,2,1,0:T(8,128)(2,1)} %bitcast.4, f32[4,512]{1,0:T(4,128)} %bias_hbm.1, f32[4,512]{1,0:T(4,128)} %gamma_hbm.1, f32[4,512]{1,0:T(4,128)} %beta_hbm.1), custom_call_target="tpu_custom_call" | custom-call | tf_op jit(solution)/shard_map/decoder_blocks/pallas_call | solution.py:305
  94.8 1.0 %copy.7 = bf16[2,6,96,512]{3,2,1,0:T(8,128)(2,1)} copy(bf16[2,6,96,512]{3,2,1,0:T(8,128)(2,1)S(1)} %bitcast.3) | data formatting | bytes 2359296
